TPU v7x, 32 devices: a whole 2x2x4 slice. The times are simulated.
32 devices in a mesh: fsdp: 4 (over y, core), sp: 8 (over z, x).
Axes of the slice: x: 2, y: 2, z: 4, core: 2. Of those that a mesh axis runs over, the one named last changes fastest.
Arguments:
- hidden: bfloat16 [4, 2048, 5120], P('fsdp', 'sp'), may hold values from -6 to 6
- queries: bfloat16 [4, 2048, 4096], P('fsdp', 'sp'), may hold values from -240 to 240
- norm_gain: float32 [5120], replicated, may hold values from 0.5 to 1.5
- kv_weight: bfloat16 [5120, 2048], P('fsdp'), may hold values from -0.078125 to 0.078125
- value_bias: float32 [1024], replicated, may hold values from -3 to 3
- doc_lengths: int32 [4, 16], P('fsdp'), may hold values from 1 to 512, 2048 in all within a row
Outputs:
- attended: bfloat16 [4, 2048, 4096], P('fsdp', 'sp')
Inputs may be any that keep to these rules, and one draw needn't show every extreme that they name: `doc_lengths`: each row sums to 2048 and its largest entry is 512.
All inputs are finite; a program needn't handle non-finite values.
Results may differ from a plain program's by a relative error of at most 0.0067.
Values may be sent and summed in bfloat16 or wider, within the bound.
A program may use at most 128 MiB of HBM per device.

v0:
```python
import functools
import math

import jax
import jax.numpy as jnp
from jax import lax
from jax.experimental import pallas as pl
from jax.experimental.pallas import tpu as pltpu
from jax.sharding import PartitionSpec as P

QH = 32
KVH = 8
HD = 128
EPS = 1e-06
PAIR = 2 * HD
PAIRS = KVH // 2
MSGS = 2 * KVH
XCH = 8
QB = 128
MASKED = -1e30


def kernel(
    n, s, reach,
    x_hbm, q_hbm, gain_hbm, w_hbm, vbias_hbm, docs,
    out,
    x, q, gain, vbias, w, xs, xr, own, ps, pr, kv, mask,
    local_sem, x_sem, wsem, xsend, xrecv, psend, precv, ssend, srecv, fsend,
):
    tokens, depth = x.shape
    chips = n // 2
    rows = w_hbm.shape[0]
    half = 2 * rows
    mine = lax.axis_index("fsdp")
    i = lax.axis_index("sp")
    core = lax.rem(mine, 2)
    chip = mine // 2
    mate = chip * 2 + (1 - core)
    step = tokens // XCH

    barrier = pltpu.get_barrier_semaphore()
    pl.semaphore_signal(barrier, inc=1, device_id={"fsdp": mate})
    for o in range(1, chips):
        peer = lax.rem(chip + o, chips) * 2 + core
        pl.semaphore_signal(barrier, inc=1, device_id={"fsdp": peer})
    for b in range(1, reach + 1):
        @pl.when(i >= b)
        def _():
            pl.semaphore_signal(barrier, inc=1, device_id={"sp": i - b})

        @pl.when(i + b < s)
        def _():
            pl.semaphore_signal(barrier, inc=1, device_id={"sp": i + b})

    def xcopy(c):
        part = pl.ds(c * step, step)
        return pltpu.make_async_copy(x_hbm.at[part], x.at[part], x_sem.at[c])

    gcopy = pltpu.make_async_copy(gain_hbm, gain, local_sem.at[0])
    gcopy.start()
    for c in range(XCH):
        xcopy(c).start()
    wcopy = pltpu.make_async_copy(w_hbm, w.at[core], local_sem.at[1])
    qcopy = pltpu.make_async_copy(q_hbm, q, local_sem.at[2])
    bcopy = pltpu.make_async_copy(vbias_hbm, vbias, local_sem.at[3])

    def wsend():
        return pltpu.make_async_remote_copy(
            w_hbm, w.at[core], wsem.at[0], wsem.at[1], device_id={"fsdp": mate}
        )

    def xsendcopy(o, c):
        target = lax.rem(chip + o, chips)
        part = pl.ds(c * step, step)
        return pltpu.make_async_remote_copy(
            xs.at[target, part], xr.at[o - 1, part], xsend.at[o - 1, c], xrecv.at[o - 1, c],
            device_id={"fsdp": target * 2 + core},
        )

    gcopy.wait()
    for c in range(XCH):
        xcopy(c).wait()
        part = slice(c * step, (c + 1) * step)
        wide = x[part, :].astype(jnp.float32)
        inv = lax.rsqrt(jnp.mean(wide * wide, axis=-1, keepdims=True) + EPS)
        for t in range(chips):
            piece = x[part, t * half:(t + 1) * half].astype(jnp.float32)
            piece = piece * inv * gain[:, t * half:(t + 1) * half]
            xs[t, part, :] = piece.astype(jnp.bfloat16)
        if c == 0:
            near = jnp.minimum(i, reach) + jnp.minimum(s - 1 - i, reach)
            pl.semaphore_wait(barrier, chips + near)
        for o in range(1, chips):
            xsendcopy(o, c).start()
        if c == 0:
            wsend().start()
            wcopy.start()
            bcopy.start()
            qcopy.start()

    first = i * tokens
    width = reach * tokens + QB
    for u in range(tokens // QB):
        pos = first + u * QB + lax.broadcasted_iota(jnp.int32, (QB, 1), 0)
        start = jnp.zeros((QB, 1), jnp.int32)
        end = jnp.int32(0)
        for d in range(docs.shape[1]):
            end = end + docs[0, d]
            start = jnp.where(pos >= end, end, start)
        key = first + u * QB - reach * tokens + lax.broadcasted_iota(jnp.int32, (QB, width), 1)
        mask[u] = jnp.where((key >= start) & (key <= pos), 0.0, MASKED)
    for b in range(1, reach + 1):
        @pl.when(i < b)
        def _():
            kv[:, (reach - b) * tokens:(reach - b + 1) * tokens, :] = jnp.zeros(
                (MSGS, tokens, HD), jnp.bfloat16
            )

    def project(left, j, kind):
        cols = pl.ds(pl.multiple_of(kind * (KVH * HD) + j * PAIR, PAIR), PAIR)
        total = jnp.dot(left[:, :rows], w[0, :, cols], preferred_element_type=jnp.float32)
        return total + jnp.dot(
            left[:, rows:], w[1, :, cols], preferred_element_type=jnp.float32
        )

    wcopy.wait()
    wsend().wait()
    bcopy.wait()
    qcopy.wait()

    @pl.loop(0, PAIRS)
    def _(j):
        keys = project(xs.at[chip], j, 0)
        values = project(xs.at[chip], j, 1)
        values = values + vbias[:, pl.ds(pl.multiple_of(j * PAIR, PAIR), PAIR)]
        for h in range(2):
            own[4 * j + 2 * h] = keys[:, h * HD:(h + 1) * HD]
            own[4 * j + 2 * h + 1] = values[:, h * HD:(h + 1) * HD]

    def psendcopy(o, m, part):
        source = lax.rem(chip + chips - o, chips)
        return pltpu.make_async_remote_copy(
            ps.at[o - 1, m, part], pr.at[o - 1, m, part], psend.at[o - 1, m], precv.at[o - 1, m],
            device_id={"fsdp": source * 2 + core},
        )

    whole = pl.ds(0, tokens)

    def give_back(o, j, part):
        for kind in range(2):
            partial = project(xr.at[o - 1, part], j, kind).astype(jnp.bfloat16)
            for h in range(2):
                ps[o - 1, 4 * j + 2 * h + kind, part, :] = partial[:, h * HD:(h + 1) * HD]
        for m in range(4):
            psendcopy(o, 4 * j + m, part).start()

    ahead = XCH - 2
    early = pl.ds(0, ahead * step)
    late = pl.ds(ahead * step, tokens - ahead * step)
    for o in range(1, chips):
        for c in range(ahead):
            xsendcopy(o, c).wait_recv()
        give_back(o, 0, early)
    for o in range(1, chips):
        for c in range(ahead, XCH):
            xsendcopy(o, c).wait_recv()
        give_back(o, 0, late)

    @pl.loop(1, PAIRS)
    def _(j):
        for o in range(1, chips):
            give_back(o, j, whole)

    def slot(b):
        return pl.ds((reach - b) * tokens, tokens)

    def shiftcopy(b, m):
        return pltpu.make_async_remote_copy(
            kv.at[m, slot(0)], kv.at[m, slot(b)], ssend.at[b - 1, m], srecv.at[b - 1, m],
            device_id={"sp": i + b},
        )

    def relay(m):
        return pltpu.make_async_remote_copy(
            kv.at[m, slot(2)], kv.at[m, slot(1)], fsend.at[m], srecv.at[0, m],
            device_id={"sp": i - 1},
        )

    odd = lax.rem(i, 2) == 1

    def sends(b):
        return (i + b < s) & jnp.logical_not(odd) if b == 1 else i + b < s

    def finish(m):
        total = own[m]
        for o in range(1, chips):
            psendcopy(o, m, whole).wait_recv()
            total = total + pr[o - 1, m].astype(jnp.float32)
        kv[m, reach * tokens:, :] = total.astype(jnp.bfloat16)
        for b in range(reach, 0, -1):
            @pl.when(sends(b))
            def _():
                shiftcopy(b, m).start()

    def pass_on(m):
        @pl.when(i >= 2)
        def _():
            shiftcopy(2, m).wait_recv()

        @pl.when(odd & (i >= 3))
        def _():
            relay(m).start()

    def arrive(m):
        for b in range(1, reach + 1):
            if b != 2:
                @pl.when(i >= b)
                def _():
                    shiftcopy(b, m).wait_recv()

    factor = HD ** (-0.5) * math.log2(math.e)
    ratio = QH // KVH

    def attend(g):
        base = pl.multiple_of(g * ratio * HD, HD)
        for u in range(tokens // QB):
            left = jnp.concatenate(
                [q[u * QB:(u + 1) * QB, pl.ds(base + r * HD, HD)] for r in range(ratio)], 0
            )
            keys = kv[2 * g, u * QB:u * QB + width, :]
            values = kv[2 * g + 1, u * QB:u * QB + width, :]
            scores = lax.dot_general(
                left, keys, (((1,), (1,)), ((), ())), preferred_element_type=jnp.float32
            )
            scores = scores.reshape(ratio, QB, width) + mask[u][None]
            scores = scores.reshape(ratio * QB, width)
            highest = jnp.max(scores, axis=-1, keepdims=True)
            probs = jnp.exp2((scores - highest) * factor)
            total = jnp.sum(probs, axis=-1, keepdims=True)
            result = jnp.dot(
                probs.astype(jnp.bfloat16), values, preferred_element_type=jnp.float32
            )
            result = (result / total).astype(jnp.bfloat16)
            for r in range(ratio):
                out[u * QB:(u + 1) * QB, pl.ds(base + r * HD, HD)] = result[
                    r * QB:(r + 1) * QB
                ]

    @pl.loop(0, KVH + 2)
    def _(t):
        for kind in range(2):
            @pl.when(t < KVH)
            def _():
                finish(2 * t + kind)

            @pl.when((t >= 1) & (t < KVH + 1))
            def _():
                pass_on(2 * t - 2 + kind)

        @pl.when(t >= 2)
        def _():
            arrive(2 * t - 4)
            arrive(2 * t - 3)
            attend(t - 2)

    for o in range(1, chips):
        for c in range(XCH):
            xsendcopy(o, c).wait_send()

    @pl.loop(0, MSGS)
    def _(m):
        for o in range(1, chips):
            psendcopy(o, m, whole).wait_send()
        for b in range(1, reach + 1):
            @pl.when(sends(b))
            def _():
                shiftcopy(b, m).wait_send()

        @pl.when(odd & (i >= 3))
        def _():
            relay(m).wait_send()


def shards(n, s, hidden, queries, norm_gain, kv_weight, value_bias, doc_lengths):
    _, tokens, depth = hidden.shape
    reach = s // 4
    chips = n // 2
    rows = kv_weight.shape[0]
    far = chips - 1
    vmem = pltpu.VMEM
    dma = pltpu.SemaphoreType.DMA
    anywhere = pl.BlockSpec(memory_space=pltpu.HBM)
    result = pl.pallas_call(
        functools.partial(kernel, n, s, reach),
        out_shape=jax.ShapeDtypeStruct((tokens, QH * HD), jnp.bfloat16),
        in_specs=[anywhere] * 5 + [pl.BlockSpec(memory_space=pltpu.SMEM)],
        out_specs=pl.BlockSpec(memory_space=pltpu.VMEM),
        scratch_shapes=[
            vmem((tokens, depth), jnp.bfloat16),
            vmem((tokens, QH * HD), jnp.bfloat16),
            vmem((1, depth), jnp.float32),
            vmem((1, KVH * HD), jnp.float32),
            vmem((2, rows, 2 * KVH * HD), jnp.bfloat16),
            vmem((chips, tokens, 2 * rows), jnp.bfloat16),
            vmem((far, tokens, 2 * rows), jnp.bfloat16),
            vmem((MSGS, tokens, HD), jnp.float32),
            vmem((far, MSGS, tokens, HD), jnp.bfloat16),
            vmem((far, MSGS, tokens, HD), jnp.bfloat16),
            vmem((MSGS, (reach + 1) * tokens, HD), jnp.bfloat16),
            vmem((tokens // QB, QB, reach * tokens + QB), jnp.float32),
            dma((4,)),
            dma((XCH,)),
            dma((2,)),
            dma((far, XCH)),
            dma((far, XCH)),
            dma((far, MSGS)),
            dma((far, MSGS)),
            dma((reach, MSGS)),
            dma((reach, MSGS)),
            dma((MSGS,)),
        ],
        compiler_params=pltpu.CompilerParams(
            collective_id=0, has_side_effects=True, vmem_limit_bytes=50 * 1024 * 1024
        ),
    )(
        hidden[0], queries[0], norm_gain.reshape(1, depth), kv_weight,
        value_bias.reshape(1, KVH * HD), doc_lengths,
    )
    return result.reshape(1, tokens, QH * HD)


def solution(mesh):
    in_specs = (
        P("fsdp", "sp", None),
        P("fsdp", "sp", None),
        P(),
        P("fsdp", None),
        P(),
        P("fsdp", None),
    )
    body = functools.partial(shards, mesh.shape["fsdp"], mesh.shape["sp"])
    return jax.shard_map(
        body, mesh=mesh, in_specs=in_specs, out_specs=P("fsdp", "sp", None), check_vma=False
    )
```

profile of v0, /device:TPU:8, one launch (start us, length us, event | category | flops | bytes accessed | tf_op | source)
XLA Modules:
  0.0 70.9 jit_solution(8885063265529638245)
XLA Ops:
  0.0 0.0 copy-start
  0.0 0.7 %copy-done = f32[5120]{0:T(1024)S(1)} copy-done((f32[5120]{0:T(1024)S(1)}, f32[5120]{0:T(1024)}, u32[]{:S(2)}) %copy-start) | copy-done | bytes 20504
  0.7 0.0 copy-start.1
  0.7 0.7 copy-done.1
  1.4 0.0 copy-start.2
  1.4 0.7 copy-done.2
  2.1 67.5 %shard_map.64 = bf16[256,4096]{1,0:T(8,128)(2,1)S(1)} custom-call(bf16[256,5120]{1,0:T(8,128)(2,1)} %bitcast.8, bf16[256,4096]{1,0:T(8,128)(2,1)} %bitcast.9, f32[1,5120]{1,0:T(1,128)S(1)} %bitcast.6, bf16[1280,2048]{1,0:T(8,128)(2,1)} %w_hbm.1, f32[1,1024]{1,0:T(1,128)S(1)} %bitcast.7, s32[1,16]{1,0:T(1,128)S(1)} %copy-done.2), custom_call_target="tpu_custom_call" | custom-call | tf_op jit(solution)/shard_map/pallas_call | solution.py:293
  69.6 1.3 %copy.8 = bf16[1,256,4096]{2,1,0:T(8,128)(2,1)} copy(bf16[1,256,4096]{2,1,0:T(8,128)(2,1)S(1)} %bitcast.5) | data formatting | bytes 4194304
Async XLA Ops:
  0.0 0.7 %copy-start = (f32[5120]{0:T(1024)S(1)}, f32[5120]{0:T(1024)}, u32[]{:S(2)}) copy-start(f32[5120]{0:T(1024)} %param.8) | copy-start | bytes 61444
  0.7 0.7 copy-start.1
  1.4 0.7 copy-start.2
where the time goes:
time: 72.3 us; the launch traced here: 70.9 us
  Pallas kernels  67.5 us (93%)
  local copies, waits for them, and re-layouts  3.39 us (5%)
    pallas_call x1, Pallas kernels, shards(): pl.pallas_call(functools.partial(kernel, n, s, reach), out_shape=jax.Shap...  67.5 us
    unnamed x7, local copies, waits for them, and re-layouts  3.39 us

commit v1 on v0

--- a/solution.py
+++ b/solution.py
@@ -15,6 +15,8 @@
 PAIR = 2 * HD
 PAIRS = KVH // 2
 MSGS = 2 * KVH
+LAST = MSGS - 2
+SEATS = MSGS + 2
 XCH = 8
 QB = 128
 MASKED = -1e30
@@ -22,9 +24,9 @@
 
 def kernel(
     n, s, reach,
-    x_hbm, q_hbm, gain_hbm, w_hbm, vbias_hbm, docs,
+    x_hbm, q_hbm, gain_hbm, w_hbm, vbias_hbm, docs_hbm,
     out,
-    x, q, gain, vbias, w, xs, xr, own, ps, pr, kv, mask,
+    docs, x, q, gain, vbias, w, xs, xr, own, ps, pr, kv, mask,
     local_sem, x_sem, wsem, xsend, xrecv, psend, precv, ssend, srecv, fsend,
 ):
     tokens, depth = x.shape
@@ -58,6 +60,8 @@
 
     gcopy = pltpu.make_async_copy(gain_hbm, gain, local_sem.at[0])
     gcopy.start()
+    dcopy = pltpu.make_async_copy(docs_hbm, docs, local_sem.at[4])
+    dcopy.start()
     for c in range(XCH):
         xcopy(c).start()
     wcopy = pltpu.make_async_copy(w_hbm, w.at[core], local_sem.at[1])
@@ -78,6 +82,7 @@
         )
 
     gcopy.wait()
+    dcopy.wait()
     for c in range(XCH):
         xcopy(c).wait()
         part = slice(c * step, (c + 1) * step)
@@ -137,14 +142,16 @@
             own[4 * j + 2 * h] = keys[:, h * HD:(h + 1) * HD]
             own[4 * j + 2 * h + 1] = values[:, h * HD:(h + 1) * HD]
 
-    def psendcopy(o, m, part):
+    def psendcopy(o, m, part, k):
         source = lax.rem(chip + chips - o, chips)
         return pltpu.make_async_remote_copy(
-            ps.at[o - 1, m, part], pr.at[o - 1, m, part], psend.at[o - 1, m], precv.at[o - 1, m],
+            ps.at[o - 1, m, part], pr.at[o - 1, m, part], psend.at[o - 1, k], precv.at[o - 1, k],
             device_id={"fsdp": source * 2 + core},
         )
 
     whole = pl.ds(0, tokens)
+    half_tokens = tokens // 2
+    pieces = (pl.ds(0, half_tokens), pl.ds(half_tokens, half_tokens))
 
     def give_back(o, j, part):
         for kind in range(2):
@@ -152,7 +159,11 @@
             for h in range(2):
                 ps[o - 1, 4 * j + 2 * h + kind, part, :] = partial[:, h * HD:(h + 1) * HD]
         for m in range(4):
-            psendcopy(o, 4 * j + m, part).start()
+            if isinstance(j, int) and j == PAIRS - 1 and m >= 2:
+                for piece in range(2):
+                    psendcopy(o, 4 * j + m, pieces[piece], 4 * j + m + 2 * piece).start()
+            else:
+                psendcopy(o, 4 * j + m, part, 4 * j + m).start()
 
     ahead = XCH - 2
     early = pl.ds(0, ahead * step)
@@ -166,23 +177,37 @@
             xsendcopy(o, c).wait_recv()
         give_back(o, 0, late)
 
-    @pl.loop(1, PAIRS)
+    @pl.loop(1, PAIRS - 1)
     def _(j):
         for o in range(1, chips):
             give_back(o, j, whole)
 
-    def slot(b):
-        return pl.ds((reach - b) * tokens, tokens)
-
-    def shiftcopy(b, m):
+    for o in range(1, chips):
+        give_back(o, PAIRS - 1, whole)
+
+    def rows_of(piece):
+        return whole if piece is None else pieces[piece]
+
+    def seat(m, piece):
+        return m if piece is None else m + 2 * piece
+
+    def slot(b, piece=None):
+        base = (reach - b) * tokens
+        if piece is None:
+            return pl.ds(base, tokens)
+        return pl.ds(base + piece * half_tokens, half_tokens)
+
+    def shiftcopy(b, m, piece=None):
+        k = seat(m, piece)
         return pltpu.make_async_remote_copy(
-            kv.at[m, slot(0)], kv.at[m, slot(b)], ssend.at[b - 1, m], srecv.at[b - 1, m],
-            device_id={"sp": i + b},
-        )
-
-    def relay(m):
+            kv.at[m, slot(0, piece)], kv.at[m, slot(b, piece)], ssend.at[b - 1, k],
+            srecv.at[b - 1, k], device_id={"sp": i + b},
+        )
+
+    def relay(m, piece=None):
+        k = seat(m, piece)
         return pltpu.make_async_remote_copy(
-            kv.at[m, slot(2)], kv.at[m, slot(1)], fsend.at[m], srecv.at[0, m],
+            kv.at[m, slot(2, piece)], kv.at[m, slot(1, piece)], fsend.at[k], srecv.at[0, k],
             device_id={"sp": i - 1},
         )
 
@@ -191,94 +216,124 @@
     def sends(b):
         return (i + b < s) & jnp.logical_not(odd) if b == 1 else i + b < s
 
-    def finish(m):
-        total = own[m]
+    def finish(m, piece=None):
+        rows_m = rows_of(piece)
+        total = own[m, rows_m]
         for o in range(1, chips):
-            psendcopy(o, m, whole).wait_recv()
-            total = total + pr[o - 1, m].astype(jnp.float32)
-        kv[m, reach * tokens:, :] = total.astype(jnp.bfloat16)
+            psendcopy(o, m, rows_m, seat(m, piece)).wait_recv()
+            total = total + pr[o - 1, m, rows_m].astype(jnp.float32)
+        kv[m, slot(0, piece), :] = total.astype(jnp.bfloat16)
         for b in range(reach, 0, -1):
             @pl.when(sends(b))
             def _():
-                shiftcopy(b, m).start()
-
-    def pass_on(m):
+                shiftcopy(b, m, piece).start()
+
+    def pass_on(m, piece=None):
         @pl.when(i >= 2)
         def _():
-            shiftcopy(2, m).wait_recv()
+            shiftcopy(2, m, piece).wait_recv()
 
         @pl.when(odd & (i >= 3))
         def _():
-            relay(m).start()
-
-    def arrive(m):
+            relay(m, piece).start()
+
+    def arrive(m, piece=None):
         for b in range(1, reach + 1):
             if b != 2:
                 @pl.when(i >= b)
                 def _():
-                    shiftcopy(b, m).wait_recv()
+                    shiftcopy(b, m, piece).wait_recv()
 
     factor = HD ** (-0.5) * math.log2(math.e)
     ratio = QH // KVH
 
-    def attend(g):
-        base = pl.multiple_of(g * ratio * HD, HD)
-        for u in range(tokens // QB):
-            left = jnp.concatenate(
-                [q[u * QB:(u + 1) * QB, pl.ds(base + r * HD, HD)] for r in range(ratio)], 0
-            )
-            keys = kv[2 * g, u * QB:u * QB + width, :]
-            values = kv[2 * g + 1, u * QB:u * QB + width, :]
-            scores = lax.dot_general(
-                left, keys, (((1,), (1,)), ((), ())), preferred_element_type=jnp.float32
-            )
-            scores = scores.reshape(ratio, QB, width) + mask[u][None]
-            scores = scores.reshape(ratio * QB, width)
-            highest = jnp.max(scores, axis=-1, keepdims=True)
-            probs = jnp.exp2((scores - highest) * factor)
-            total = jnp.sum(probs, axis=-1, keepdims=True)
-            result = jnp.dot(
-                probs.astype(jnp.bfloat16), values, preferred_element_type=jnp.float32
-            )
-            result = (result / total).astype(jnp.bfloat16)
-            for r in range(ratio):
-                out[u * QB:(u + 1) * QB, pl.ds(base + r * HD, HD)] = result[
-                    r * QB:(r + 1) * QB
-                ]
-
-    @pl.loop(0, KVH + 2)
+    def attend(g, u):
+        base = g * ratio * HD
+        if not isinstance(g, int):
+            base = pl.multiple_of(base, HD)
+        left = jnp.concatenate(
+            [q[u * QB:(u + 1) * QB, pl.ds(base + r * HD, HD)] for r in range(ratio)], 0
+        )
+        keys = kv[2 * g, u * QB:u * QB + width, :]
+        values = kv[2 * g + 1, u * QB:u * QB + width, :]
+        scores = lax.dot_general(
+            left, keys, (((1,), (1,)), ((), ())), preferred_element_type=jnp.float32
+        )
+        scores = scores.reshape(ratio, QB, width) + mask[u][None]
+        scores = scores.reshape(ratio * QB, width)
+        highest = jnp.max(scores, axis=-1, keepdims=True)
+        probs = jnp.exp2((scores - highest) * factor)
+        total = jnp.sum(probs, axis=-1, keepdims=True)
+        result = jnp.dot(
+            probs.astype(jnp.bfloat16), values, preferred_element_type=jnp.float32
+        )
+        result = (result / total).astype(jnp.bfloat16)
+        for r in range(ratio):
+            out[u * QB:(u + 1) * QB, pl.ds(base + r * HD, HD)] = result[
+                r * QB:(r + 1) * QB
+            ]
+
+    def when(condition, action):
+        @pl.when(condition)
+        def _():
+            action()
+
+    def opening(g):
+        arrive(2 * g)
+        arrive(2 * g + 1)
+        attend(g, 0)
+
+    @pl.loop(0, KVH - 1)
     def _(t):
-        for kind in range(2):
-            @pl.when(t < KVH)
-            def _():
-                finish(2 * t + kind)
-
-            @pl.when((t >= 1) & (t < KVH + 1))
-            def _():
-                pass_on(2 * t - 2 + kind)
-
-        @pl.when(t >= 2)
-        def _():
-            arrive(2 * t - 4)
-            arrive(2 * t - 3)
-            attend(t - 2)
+        finish(2 * t)
+        when(t >= 2, lambda: pass_on(2 * t - 3))
+        when(t >= 4, lambda: attend(t - 4, 1))
+        finish(2 * t + 1)
+        when(t >= 1, lambda: pass_on(2 * t - 2))
+        when(t >= 3, lambda: opening(t - 3))
+
+    finish(LAST, 0)
+    pass_on(LAST - 3)
+    attend(KVH - 5, 1)
+    finish(LAST, 1)
+    finish(LAST + 1, 0)
+    pass_on(LAST - 2)
+    opening(KVH - 4)
+    finish(LAST + 1, 1)
+    pass_on(LAST - 1)
+    pass_on(LAST, 0)
+    attend(KVH - 4, 1)
+    pass_on(LAST, 1)
+    opening(KVH - 3)
+    pass_on(LAST + 1, 0)
+    pass_on(LAST + 1, 1)
+    attend(KVH - 3, 1)
+    opening(KVH - 2)
+    attend(KVH - 2, 1)
+    for piece in range(2):
+        arrive(LAST, piece)
+        arrive(LAST + 1, piece)
+    attend(KVH - 1, 0)
+    attend(KVH - 1, 1)
 
     for o in range(1, chips):
         for c in range(XCH):
             xsendcopy(o, c).wait_send()
 
-    @pl.loop(0, MSGS)
+    def settle(m, piece=None):
+        for o in range(1, chips):
+            psendcopy(o, m, rows_of(piece), seat(m, piece)).wait_send()
+        for b in range(1, reach + 1):
+            when(sends(b), lambda: shiftcopy(b, m, piece).wait_send())
+        when(odd & (i >= 3), lambda: relay(m, piece).wait_send())
+
+    @pl.loop(0, LAST)
     def _(m):
-        for o in range(1, chips):
-            psendcopy(o, m, whole).wait_send()
-        for b in range(1, reach + 1):
-            @pl.when(sends(b))
-            def _():
-                shiftcopy(b, m).wait_send()
-
-        @pl.when(odd & (i >= 3))
-        def _():
-            relay(m).wait_send()
+        settle(m)
+
+    for piece in range(2):
+        settle(LAST, piece)
+        settle(LAST + 1, piece)
 
 
 def shards(n, s, hidden, queries, norm_gain, kv_weight, value_bias, doc_lengths):
@@ -289,13 +344,15 @@
     far = chips - 1
     vmem = pltpu.VMEM
     dma = pltpu.SemaphoreType.DMA
+    hold = lambda a: pltpu.with_memory_space_constraint(a, pltpu.HBM)
     anywhere = pl.BlockSpec(memory_space=pltpu.HBM)
     result = pl.pallas_call(
         functools.partial(kernel, n, s, reach),
         out_shape=jax.ShapeDtypeStruct((tokens, QH * HD), jnp.bfloat16),
-        in_specs=[anywhere] * 5 + [pl.BlockSpec(memory_space=pltpu.SMEM)],
+        in_specs=[anywhere] * 6,
         out_specs=pl.BlockSpec(memory_space=pltpu.VMEM),
         scratch_shapes=[
+            pltpu.SMEM((1, doc_lengths.shape[1]), jnp.int32),
             vmem((tokens, depth), jnp.bfloat16),
             vmem((tokens, QH * HD), jnp.bfloat16),
             vmem((1, depth), jnp.float32),
@@ -308,23 +365,23 @@
             vmem((far, MSGS, tokens, HD), jnp.bfloat16),
             vmem((MSGS, (reach + 1) * tokens, HD), jnp.bfloat16),
             vmem((tokens // QB, QB, reach * tokens + QB), jnp.float32),
-            dma((4,)),
+            dma((5,)),
             dma((XCH,)),
             dma((2,)),
             dma((far, XCH)),
             dma((far, XCH)),
-            dma((far, MSGS)),
-            dma((far, MSGS)),
-            dma((reach, MSGS)),
-            dma((reach, MSGS)),
-            dma((MSGS,)),
+            dma((far, SEATS)),
+            dma((far, SEATS)),
+            dma((reach, SEATS)),
+            dma((reach, SEATS)),
+            dma((SEATS,)),
         ],
         compiler_params=pltpu.CompilerParams(
             collective_id=0, has_side_effects=True, vmem_limit_bytes=50 * 1024 * 1024
         ),
     )(
-        hidden[0], queries[0], norm_gain.reshape(1, depth), kv_weight,
-        value_bias.reshape(1, KVH * HD), doc_lengths,
+        hidden[0], queries[0], hold(norm_gain.reshape(1, depth)), kv_weight,
+        hold(value_bias.reshape(1, KVH * HD)), hold(doc_lengths),
     )
     return result.reshape(1, tokens, QH * HD)
 

time: 72.3 us -> 68.5 us (0.947); the launches traced: 70.9 us -> 68.1 us
  local copies, waits for them, and re-layouts: 3.39 us -> 1.32 us
    unnamed x7 -> x1, local copies, waits for them, and re-layouts: 3.39 us -> 1.32 us
    pallas_call x1, Pallas kernels: 67.5 us -> 66.8 us  [shards(): pl.pallas_call(functools.partial(kernel, n, s, reach), out_shape=jax.Shap...]
where the time goes in v1:
time: 68.5 us; the launch traced here: 68.1 us
  Pallas kernels  66.8 us (98%)
  local copies, waits for them, and re-layouts  1.32 us (2%)
    pallas_call x1, Pallas kernels, shards(): pl.pallas_call(functools.partial(kernel, n, s, reach), out_shape=jax.Shap...  66.8 us

profile of v1, /device:TPU:8, one launch (start us, length us, event | category | flops | bytes accessed | tf_op | source)
XLA Modules:
  0.0 68.1 jit_solution(9728713093731229283)
XLA Ops:
  0.0 66.8 %shard_map.64 = bf16[256,4096]{1,0:T(8,128)(2,1)S(1)} custom-call(bf16[256,5120]{1,0:T(8,128)(2,1)} %bitcast.6, bf16[256,4096]{1,0:T(8,128)(2,1)} %bitcast.7, f32[1,5120]{1,0:T(1,128)} %bitcast.8, bf16[1280,2048]{1,0:T(8,128)(2,1)} %w_hbm.1, f32[1,1024]{1,0:T(1,128)} %bitcast.9, s32[1,16]{1,0:T(1,128)} %docs_hbm.1), custom_call_target="tpu_custom_call" | custom-call | tf_op jit(solution)/shard_map/pallas_call | solution.py:349
  66.8 1.3 %copy.8 = bf16[1,256,4096]{2,1,0:T(8,128)(2,1)} copy(bf16[1,256,4096]{2,1,0:T(8,128)(2,1)S(1)} %bitcast.5) | data formatting | bytes 4194304

commit v2 on v1

v2 whole, which is shorter than its diff:
```python
import functools
import math

import jax
import jax.numpy as jnp
from jax import lax
from jax.experimental import pallas as pl
from jax.experimental.pallas import tpu as pltpu
from jax.sharding import PartitionSpec as P

QH = 32
KVH = 8
HD = 128
EPS = 1e-06
PAIR = 2 * HD
PAIRS = KVH // 2
MSGS = 2 * KVH
LAST = MSGS - 2
SPLIT = 4
SEATS = MSGS + 2 + SPLIT
FIRST, SECOND, EARLY, LATE = range(4)
XCH = 8
QB = 128
MASKED = -1e30
SHARE = 3
PARTS = 2


def aligned(index, step):
    return index if isinstance(index, int) else pl.multiple_of(index, step)


def kernel(
    n, s, reach, give,
    x_hbm, q_hbm, gain_hbm, w_hbm, vbias_hbm, docs_hbm,
    out,
    docs, x, q, res, gain, vbias, w, xs, xr, own, ps, pr, kv, mask,
    local_sem, x_sem, wsem, xsend, xrecv, psend, precv, ssend, srecv, fsend, osem,
    *gather,
):
    tokens, depth = x.shape
    chips = n // 2
    rows = w_hbm.shape[0]
    half = 2 * rows
    kept = rows - give
    sent = 2 * kept
    mine = lax.axis_index("fsdp")
    i = lax.axis_index("sp")
    core = lax.rem(mine, 2)
    chip = mine // 2
    mate = chip * 2 + (1 - core)
    step = tokens // XCH

    barrier = pltpu.get_barrier_semaphore()
    pl.semaphore_signal(barrier, inc=1, device_id={"fsdp": mate})
    for o in range(1, chips):
        peer = lax.rem(chip + o, chips) * 2 + core
        pl.semaphore_signal(barrier, inc=1, device_id={"fsdp": peer})
    if give:
        for o in range(1, s):
            pl.semaphore_signal(barrier, inc=1, device_id={"sp": lax.rem(i + o, s)})
        callers = chips + s - 1
    else:
        for b in range(1, reach + 1):
            @pl.when(i >= b)
            def _():
                pl.semaphore_signal(barrier, inc=1, device_id={"sp": i - b})

            @pl.when(i + b < s)
            def _():
                pl.semaphore_signal(barrier, inc=1, device_id={"sp": i + b})
        callers = chips + jnp.minimum(i, reach) + jnp.minimum(s - 1 - i, reach)

    def take(sem, ref):
        pltpu.make_async_copy(ref, ref, sem).wait()

    def xcopy(c):
        part = pl.ds(c * step, step)
        return pltpu.make_async_copy(x_hbm.at[part], x.at[part], x_sem.at[c])

    gcopy = pltpu.make_async_copy(gain_hbm, gain.at[:, pl.ds(0, depth)], local_sem.at[0])
    gcopy.start()
    dcopy = pltpu.make_async_copy(docs_hbm, docs, local_sem.at[4])
    dcopy.start()
    for c in range(XCH):
        xcopy(c).start()
    qcopy = pltpu.make_async_copy(q_hbm, q, local_sem.at[2])
    bcopy = pltpu.make_async_copy(vbias_hbm, vbias, local_sem.at[3])

    bands = [(pl.ds(give, kept), pl.ds(core * kept, kept))]
    if give:
        bands.append((pl.ds(0, give), pl.ds(sent + core * give, give)))

    def wcopies():
        return [
            pltpu.make_async_copy(w_hbm.at[a], w.at[b], local_sem.at[(1, 5)[k]])
            for k, (a, b) in enumerate(bands)
        ]

    def wsends():
        return [
            pltpu.make_async_remote_copy(
                w_hbm.at[a], w.at[b], wsem.at[k, 0], wsem.at[k, 1], device_id={"fsdp": mate}
            )
            for k, (a, b) in enumerate(bands)
        ]

    def xsendcopy(o, c):
        target = lax.rem(chip + o, chips)
        part = pl.ds(c * step, step)
        return pltpu.make_async_remote_copy(
            xs.at[target, part, pl.ds(0, sent)], xr.at[o - 1, part], xsend.at[o - 1],
            xrecv.at[o - 1, c // (XCH - 2)], device_id={"fsdp": target * 2 + core},
        )

    if give:
        wg, ysend, yrecv, zsend, hsend, grecv, msend, mrecv = gather
        parts, _, wide_cols = wg.shape
        strip = give // s
        lines = s // 2
        beside = i + 1 - 2 * lax.rem(i, 2)

        def slab(c, k):
            return pl.ds(pl.multiple_of(c * give + k * strip, 16), strip)

        def ygive(h, kind):
            span = wide_cols // 2
            return pltpu.make_async_remote_copy(
                w_hbm.at[pl.ds(pl.multiple_of(i * strip, 16), strip),
                         pl.ds(kind * (KVH * HD) + h * span, span)],
                wg.at[h, slab(core, i), pl.ds(kind * span, span)],
                ysend.at[h], yrecv.at[h],
                device_id={"fsdp": (1 - chip) * 2 + core},
            )

        def zgive(h, k, up):
            return pltpu.make_async_remote_copy(
                wg.at[h, slab(core, k)], wg.at[h, slab(core, k)], zsend.at[h, up],
                grecv.at[h, k], device_id={"sp": i + (2 if up else -2)},
            )

        def has(up):
            return i + 2 < s if up else i >= 2

        def hgive(h, k):
            return pltpu.make_async_remote_copy(
                wg.at[h, slab(core, k)], wg.at[h, slab(core, k)], hsend.at[h],
                grecv.at[h, k], device_id={"sp": beside},
            )

        def mgive(h, k, c):
            return pltpu.make_async_remote_copy(
                wg.at[h, slab(c, k)], wg.at[h, slab(c, k)], msend.at[h], mrecv.at[h],
                device_id={"fsdp": mate},
            )

        def spread(h):
            take(yrecv.at[h], wg.at[h, slab(core, i)])
            for up in (1, 0):
                @pl.when(has(up))
                def _():
                    zgive(h, i, up).start()
            hgive(h, i).start()
            mgive(h, i, core).start()

        def across(h, d):
            for up in (1, 0):
                k = i - 2 * d if up else i + 2 * d

                @pl.when(k >= 0 if up else k < s)
                def _():
                    hgive(h, k).wait_recv()

                    @pl.when(has(up))
                    def _():
                        zgive(h, k, up).start()

                    hgive(h, k).start()
                    mgive(h, k, core).start()

        def inward(h, o):
            k = lax.rem(beside + s - 2 * o, s)
            hgive(h, k).wait_recv()
            mgive(h, k, core).start()

        def gathered(h):
            take(mrecv.at[h], wg.at[h, pl.ds(pl.multiple_of((1 - core) * give, 16), give)])

        def regain():
            for h in range(parts):
                take(ysend.at[h], wg.at[h, pl.ds(0, strip)])
                take(hsend.at[h], wg.at[h, pl.ds(0, lines * strip)])
                take(msend.at[h], wg.at[h, pl.ds(0, give)])
                for up in (1, 0):
                    for d in range(lines - 1):
                        passed = i // 2 if up else lines - 1 - i // 2

                        @pl.when(passed == d)
                        def _():
                            take(zsend.at[h, up], wg.at[h, pl.ds(0, (d + 1) * strip)])

    pieces_of = [(0, give, kept), (kept, rows + give, kept)]
    if give:
        pieces_of += [(sent, 0, give), (sent + give, rows, give)]
    gcopy.wait()
    dcopy.wait()
    for c in range(XCH):
        xcopy(c).wait()
        part = slice(c * step, (c + 1) * step)
        wide = x[part, :].astype(jnp.float32)
        inv = lax.rsqrt(jnp.mean(wide * wide, axis=-1, keepdims=True) + EPS)
        for t in range(chips):
            for to, at, size in pieces_of:
                cut = slice(t * half + at, t * half + at + size)
                piece = x[part, cut].astype(jnp.float32) * inv * gain[:, cut]
                xs[t, part, to:to + size] = piece.astype(jnp.bfloat16)
        if c == 0:
            pl.semaphore_wait(barrier, callers)
            if give:
                for h in range(parts):
                    for kind in range(2):
                        ygive(h, kind).start()
        for o in range(1, chips):
            xsendcopy(o, c).start()
        if c == 0:
            for copy in wsends() + wcopies():
                copy.start()
            bcopy.start()
            qcopy.start()

    first = i * tokens
    width = reach * tokens + QB
    for u in range(tokens // QB):
        pos = first + u * QB + lax.broadcasted_iota(jnp.int32, (QB, 1), 0)
        start = jnp.zeros((QB, 1), jnp.int32)
        end = jnp.int32(0)
        for d in range(docs.shape[1]):
            end = end + docs[0, d]
            start = jnp.where(pos >= end, end, start)
        key = first + u * QB - reach * tokens + lax.broadcasted_iota(jnp.int32, (QB, width), 1)
        mask[u] = jnp.where((key >= start) & (key <= pos), 0.0, MASKED)
    for b in range(1, reach + 1):
        @pl.when(i < b)
        def _():
            kv[:, (reach - b) * tokens:(reach - b + 1) * tokens, :] = jnp.zeros(
                (MSGS, tokens, HD), jnp.bfloat16
            )

    def project(left, right, j, kind):
        cols = pl.ds(aligned(kind * (KVH * HD) + j * PAIR, PAIR), PAIR)
        return jnp.dot(left[...], right[:, cols], preferred_element_type=jnp.float32)

    if give:
        for h in range(parts):
            spread(h)
        across(0, 1)
    for copy in wcopies():
        copy.wait()
    for copy in wsends():
        copy.wait()
    bcopy.wait()
    qcopy.wait()

    def own_pair(j):
        keys = project(xs.at[chip], w, j, 0)
        values = project(xs.at[chip], w, j, 1)
        values = values + vbias[:, pl.ds(aligned(j * PAIR, PAIR), PAIR)]
        for h in range(2):
            own[4 * j + 2 * h] = keys[:, h * HD:(h + 1) * HD]
            own[4 * j + 2 * h + 1] = values[:, h * HD:(h + 1) * HD]

    def own_rest(j):
        left = xs[1 - chip, :, sent:]
        group = PAIRS // parts
        h = j // group
        for kind in range(2):
            cols = pl.ds((kind * group + j % group) * PAIR, PAIR)
            more = jnp.dot(left, wg[h, :, cols], preferred_element_type=jnp.float32)
            for r in range(2):
                own[4 * j + 2 * r + kind] += more[:, r * HD:(r + 1) * HD]

    if give:
        turns = [(h, d) for d in range(1, lines) for h in range(parts)][1:]
        for j in range(PAIRS):
            own_pair(j)
            for turn in turns[j:j + 1]:
                across(*turn)
        for turn in turns[PAIRS:]:
            across(*turn)
        for o in range(lines):
            inward(0, o)
    else:
        @pl.loop(0, PAIRS)
        def _(j):
            own_pair(j)

    half_tokens = tokens // 2
    ahead = (XCH - 2) * step
    spans = {
        None: (0, tokens),
        FIRST: (0, half_tokens),
        SECOND: (half_tokens, half_tokens),
        EARLY: (0, ahead),
        LATE: (ahead, tokens - ahead),
    }

    def rows_of(piece):
        return pl.ds(*spans[piece])

    def seat(m, piece):
        return m + {SECOND: 2, LATE: MSGS + 2}.get(piece, 0)

    def psendcopy(o, m, piece):
        source = lax.rem(chip + chips - o, chips)
        k = seat(m, piece)
        return pltpu.make_async_remote_copy(
            ps.at[o - 1, m, rows_of(piece)], pr.at[o - 1, m, rows_of(piece)],
            psend.at[o - 1], precv.at[o - 1, k], device_id={"fsdp": source * 2 + core},
        )

    def give_back(o, j, piece):
        part = rows_of(piece)
        for kind in range(2):
            partial = project(
                xr.at[o - 1, part], w.at[pl.ds(0, sent)], j, kind
            ).astype(jnp.bfloat16)
            for h in range(2):
                ps[o - 1, 4 * j + 2 * h + kind, part, :] = partial[:, h * HD:(h + 1) * HD]
        for m in range(4 * j, 4 * j + 4):
            for cut in (FIRST, SECOND) if m >= LAST else (piece,):
                psendcopy(o, m, cut).start()

    def slot(b, piece):
        start, size = spans[piece]
        return pl.ds((reach - b) * tokens + start, size)

    def shiftcopy(b, m, piece):
        k = seat(m, piece)
        return pltpu.make_async_remote_copy(
            kv.at[m, slot(0, piece)], kv.at[m, slot(b, piece)], ssend.at[b - 1],
            srecv.at[b - 1, k], device_id={"sp": i + b},
        )

    def relay(m, piece):
        k = seat(m, piece)
        return pltpu.make_async_remote_copy(
            kv.at[m, slot(2, piece)], kv.at[m, slot(1, piece)], fsend.at[0], srecv.at[0, k],
            device_id={"sp": i - 1},
        )

    odd = lax.rem(i, 2) == 1

    def sends(b):
        return (i + b < s) & jnp.logical_not(odd) if b == 1 else i + b < s

    def finish(m, piece):
        part = rows_of(piece)
        total = own[m, part]
        for o in range(1, chips):
            psendcopy(o, m, piece).wait_recv()
            total = total + pr[o - 1, m, part].astype(jnp.float32)
        kv[m, slot(0, piece), :] = total.astype(jnp.bfloat16)
        for b in range(reach, 0, -1):
            @pl.when(sends(b))
            def _():
                shiftcopy(b, m, piece).start()

    def pass_on(m, piece):
        @pl.when(i >= 2)
        def _():
            shiftcopy(2, m, piece).wait_recv()

        @pl.when(odd & (i >= 3))
        def _():
            relay(m, piece).start()

    def arrive(m, piece):
        for b in range(1, reach + 1):
            if b != 2:
                @pl.when(i >= b)
                def _():
                    shiftcopy(b, m, piece).wait_recv()

    factor = HD ** (-0.5) * math.log2(math.e)
    ratio = QH // KVH

    def outcopy(g, u):
        block = (
            pl.ds(u * QB, QB), pl.ds(aligned(g * ratio * HD, ratio * HD), ratio * HD)
        )
        return pltpu.make_async_copy(res.at[block], out.at[block], osem.at[0])

    def attend(g, u):
        base = aligned(g * ratio * HD, HD)
        left = jnp.concatenate(
            [q[u * QB:(u + 1) * QB, pl.ds(base + r * HD, HD)] for r in range(ratio)], 0
        )
        keys = kv[2 * g, u * QB:u * QB + width, :]
        values = kv[2 * g + 1, u * QB:u * QB + width, :]
        scores = lax.dot_general(
            left, keys, (((1,), (1,)), ((), ())), preferred_element_type=jnp.float32
        )
        scores = scores.reshape(ratio, QB, width) + mask[u][None]
        scores = scores.reshape(ratio * QB, width)
        highest = jnp.max(scores, axis=-1, keepdims=True)
        probs = jnp.exp2((scores - highest) * factor)
        total = jnp.sum(probs, axis=-1, keepdims=True)
        result = jnp.dot(
            probs.astype(jnp.bfloat16), values, preferred_element_type=jnp.float32
        )
        result = (result / total).astype(jnp.bfloat16)
        for r in range(ratio):
            res[u * QB:(u + 1) * QB, pl.ds(base + r * HD, HD)] = result[
                r * QB:(r + 1) * QB
            ]
        outcopy(g, u).start()

    def when(condition, action):
        @pl.when(condition)
        def _():
            action()

    def cuts(m):
        if m < SPLIT:
            return (EARLY, LATE)
        return (FIRST, SECOND) if m >= LAST else (None,)

    def finish_all(messages, piece):
        for m in messages:
            finish(m, piece)

    def pass_all(messages, piece):
        for m in messages:
            pass_on(m, piece)

    def first_rest():
        if give:
            for h in range(1, parts):
                for o in range(lines):
                    inward(h, o)
            gathered(0)
            for j in range(PAIRS // parts):
                own_rest(j)

    def later_rest():
        if give:
            for h in range(1, parts):
                gathered(h)
                for j in range(PAIRS // parts * h, PAIRS // parts * (h + 1)):
                    own_rest(j)

    def give_all(j, piece):
        for o in range(1, chips):
            give_back(o, j, piece)

    for o in range(1, chips):
        take(xrecv.at[o - 1, 0], xr.at[o - 1, rows_of(EARLY)])
        give_back(o, 0, EARLY)
    first_rest()
    for o in range(1, chips):
        take(xrecv.at[o - 1, 1], xr.at[o - 1, rows_of(LATE)])
        give_back(o, 0, LATE)
    for j in range(1, PAIRS):
        give_all(j, None)
        finish(j - 1, EARLY)
    later_rest()
    finish(SPLIT - 1, EARLY)
    finish_all(range(SPLIT), LATE)
    pass_all(range(SPLIT), EARLY)
    finish(SPLIT, None)
    pass_all(range(SPLIT), LATE)
    finish(SPLIT + 1, None)

    due = {}
    for g in range(4):
        for u in range(2):
            due[g, u] = ((2 * g + 6 + u, None),), ((2 * g + 4 + u, None),)
    due[4, 0] = ((LAST, FIRST), (LAST, SECOND)), ((LAST - 2, None),)
    due[4, 1] = ((LAST + 1, FIRST), (LAST + 1, SECOND)), ((LAST - 1, None),)
    due[5, 0] = (), ((LAST, FIRST),)
    due[5, 1] = (), ((LAST, SECOND), (LAST + 1, FIRST))
    due[6, 0] = (), ((LAST + 1, SECOND),)

    def serve(g, u):
        finishing, passing = due[g, u]
        for unit in finishing:
            finish(*unit)
        for unit in passing:
            pass_on(*unit)

    def ready(g):
        for m in (2 * g, 2 * g + 1):
            for cut in cuts(m):
                arrive(m, cut)

    @pl.loop(0, KVH)
    def _(g):
        for u in range(tokens // QB):
            for turn in range(KVH):
                if (turn, u) in due:
                    when(g == turn, functools.partial(serve, turn, u))
                if u == 0:
                    when(g == turn, functools.partial(ready, turn))
            attend(g, u)

    for o in range(1, chips):
        take(xsend.at[o - 1], xr.at[o - 1])
        take(psend.at[o - 1], ps.at[o - 1])
    for b in range(1, reach + 1):
        when(sends(b), functools.partial(take, ssend.at[b - 1], kv.at[:, slot(0, None)]))
    when(odd & (i >= 3), functools.partial(take, fsend.at[0], kv.at[:, slot(2, None)]))
    if give:
        regain()
    pltpu.make_async_copy(res, out, osem.at[0]).wait()


def shards(n, s, hidden, queries, norm_gain, kv_weight, value_bias, doc_lengths):
    _, tokens, depth = hidden.shape
    reach = s // 4
    chips = n // 2
    rows = kv_weight.shape[0]
    far = chips - 1
    give = rows * SHARE // 10 // HD * HD if chips == 2 and s % 2 == 0 else 0
    if give % (16 * s):
        give = 0
    kept = rows - give
    vmem = pltpu.VMEM
    dma = pltpu.SemaphoreType.DMA
    taken = [
        vmem((PARTS, 2 * give, 2 * KVH * HD // PARTS), jnp.bfloat16),
        dma((PARTS,)),
        dma((PARTS,)),
        dma((PARTS, 2)),
        dma((PARTS,)),
        dma((PARTS, s)),
        dma((PARTS,)),
        dma((PARTS,)),
    ] if give else []
    hold = lambda a: pltpu.with_memory_space_constraint(a, pltpu.HBM)
    anywhere = pl.BlockSpec(memory_space=pltpu.HBM)
    result = pl.pallas_call(
        functools.partial(kernel, n, s, reach, give),
        out_shape=jax.ShapeDtypeStruct((tokens, QH * HD), jnp.bfloat16),
        in_specs=[anywhere] * 6,
        out_specs=anywhere,
        scratch_shapes=[
            pltpu.SMEM((1, doc_lengths.shape[1]), jnp.int32),
            vmem((tokens, depth), jnp.bfloat16),
            vmem((tokens, QH * HD), jnp.bfloat16),
            vmem((tokens, QH * HD), jnp.bfloat16),
            vmem((1, depth + 8 * HD), jnp.float32),
            vmem((1, KVH * HD), jnp.float32),
            vmem((2 * rows, 2 * KVH * HD), jnp.bfloat16),
            vmem((chips, tokens, 2 * rows), jnp.bfloat16),
            vmem((far, tokens, 2 * kept), jnp.bfloat16),
            vmem((MSGS, tokens, HD), jnp.float32),
            vmem((far, MSGS, tokens, HD), jnp.bfloat16),
            vmem((far, MSGS, tokens, HD), jnp.bfloat16),
            vmem((MSGS, (reach + 1) * tokens, HD), jnp.bfloat16),
            vmem((tokens // QB, QB, reach * tokens + QB), jnp.float32),
            dma((6,)),
            dma((XCH,)),
            dma((2, 2)),
            dma((far,)),
            dma((far, 2)),
            dma((far,)),
            dma((far, SEATS)),
            dma((reach,)),
            dma((reach, SEATS)),
            dma((1,)),
            dma((1,)),
        ] + taken,
        compiler_params=pltpu.CompilerParams(
            collective_id=0, has_side_effects=True, vmem_limit_bytes=50 * 1024 * 1024
        ),
    )(
        hidden[0], queries[0], hold(norm_gain.reshape(1, depth)), kv_weight,
        hold(value_bias.reshape(1, KVH * HD)), hold(doc_lengths),
    )
    return result.reshape(1, tokens, QH * HD)


def solution(mesh):
    in_specs = (
        P("fsdp", "sp", None),
        P("fsdp", "sp", None),
        P(),
        P("fsdp", None),
        P(),
        P("fsdp", None),
    )
    body = functools.partial(shards, mesh.shape["fsdp"], mesh.shape["sp"])
    return jax.shard_map(
        body, mesh=mesh, in_specs=in_specs, out_specs=P("fsdp", "sp", None), check_vma=False
    )
```

time: 68.5 us -> 64.7 us (0.945)
  Pallas kernels: 66.8 us -> 63.1 us
    pallas_call x1, Pallas kernels: 66.8 us -> 63.1 us  [shards(): pl.pallas_call(functools.partial(kernel, n, s, reach, give), out_shape=ja...]
where the time goes in v2:
time: 64.7 us; the launch traced here: 64.4 us
  Pallas kernels  63.1 us (98%)
  local copies, waits for them, and re-layouts  1.32 us (2%)
    pallas_call x1, Pallas kernels, shards(): pl.pallas_call(functools.partial(kernel, n, s, reach, give), out_shape=ja...  63.1 us
    unnamed x1, local copies, waits for them, and re-layouts  1.32 us

profile of v2, /device:TPU:8, one launch (start us, length us, event | category | flops | bytes accessed | tf_op | source)
XLA Modules:
  0.0 64.4 jit_solution(4546976859371571817)
XLA Ops:
  0.0 63.1 %shard_map.64 = bf16[256,4096]{1,0:T(8,128)(2,1)S(1)} custom-call(bf16[256,5120]{1,0:T(8,128)(2,1)} %bitcast.6, bf16[256,4096]{1,0:T(8,128)(2,1)} %bitcast.7, f32[1,5120]{1,0:T(1,128)} %bitcast.8, bf16[1280,2048]{1,0:T(8,128)(2,1)} %w_hbm.1, f32[1,1024]{1,0:T(1,128)} %bitcast.9, s32[1,16]{1,0:T(1,128)} %docs_hbm.1), custom_call_target="tpu_custom_call" | custom-call | tf_op jit(solution)/shard_map/pallas_call | solution.py:541
  63.1 1.3 %copy.8 = bf16[1,256,4096]{2,1,0:T(8,128)(2,1)} copy(bf16[1,256,4096]{2,1,0:T(8,128)(2,1)S(1)} %bitcast.5) | data formatting | bytes 4194304

commit v3 on v2

--- a/solution.py
+++ b/solution.py
@@ -17,6 +17,8 @@
 MSGS = 2 * KVH
 LAST = MSGS - 2
 SPLIT = 4
+LEAD = 6
+NEAR = 5
 SEATS = MSGS + 2 + SPLIT
 FIRST, SECOND, EARLY, LATE = range(4)
 XCH = 8
@@ -469,38 +471,29 @@
     pass_all(range(SPLIT), EARLY)
     finish(SPLIT, None)
     pass_all(range(SPLIT), LATE)
-    finish(SPLIT + 1, None)
-
-    due = {}
-    for g in range(4):
-        for u in range(2):
-            due[g, u] = ((2 * g + 6 + u, None),), ((2 * g + 4 + u, None),)
-    due[4, 0] = ((LAST, FIRST), (LAST, SECOND)), ((LAST - 2, None),)
-    due[4, 1] = ((LAST + 1, FIRST), (LAST + 1, SECOND)), ((LAST - 1, None),)
-    due[5, 0] = (), ((LAST, FIRST),)
-    due[5, 1] = (), ((LAST, SECOND), (LAST + 1, FIRST))
-    due[6, 0] = (), ((LAST + 1, SECOND),)
-
-    def serve(g, u):
-        finishing, passing = due[g, u]
-        for unit in finishing:
-            finish(*unit)
-        for unit in passing:
-            pass_on(*unit)
+
+    def serve(k, lead, relays):
+        if k + lead < MSGS:
+            for cut in cuts(k + lead):
+                finish(k + lead, cut)
+        if relays and SPLIT <= k + lead - 3 < MSGS:
+            for cut in cuts(k + lead - 3):
+                pass_on(k + lead - 3, cut)
+
+    when(i >= 2, lambda: finish_all(range(SPLIT + 1, LEAD), None))
 
     def ready(g):
         for m in (2 * g, 2 * g + 1):
             for cut in cuts(m):
                 arrive(m, cut)
 
-    @pl.loop(0, KVH)
-    def _(g):
+    for g in range(KVH):
         for u in range(tokens // QB):
-            for turn in range(KVH):
-                if (turn, u) in due:
-                    when(g == turn, functools.partial(serve, turn, u))
-                if u == 0:
-                    when(g == turn, functools.partial(ready, turn))
+            k = g * (tokens // QB) + u
+            when(i >= 2, functools.partial(serve, k, LEAD, True))
+            when(i < 2, functools.partial(serve, k, NEAR, False))
+            if u == 0:
+                ready(g)
             attend(g, u)
 
     for o in range(1, chips):

time: 64.7 us -> 64.2 us (level)
  no operation moved by 1% of the time
where the time goes in v3:
time: 64.2 us; the launch traced here: 64 us
  Pallas kernels  62.7 us (98%)
  local copies, waits for them, and re-layouts  1.32 us (2%)
    pallas_call x1, Pallas kernels, shards(): pl.pallas_call(functools.partial(kernel, n, s, reach, give), out_shape=ja...  62.7 us
    unnamed x1, local copies, waits for them, and re-layouts  1.32 us

profile of v3, /device:TPU:8, one launch (start us, length us, event | category | flops | bytes accessed | tf_op | source)
XLA Modules:
  0.0 64.0 jit_solution(8559528953978365435)
XLA Ops:
  0.0 62.7 %shard_map.64 = bf16[256,4096]{1,0:T(8,128)(2,1)S(1)} custom-call(bf16[256,5120]{1,0:T(8,128)(2,1)} %bitcast.6, bf16[256,4096]{1,0:T(8,128)(2,1)} %bitcast.7, f32[1,5120]{1,0:T(1,128)} %bitcast.8, bf16[1280,2048]{1,0:T(8,128)(2,1)} %w_hbm.1, f32[1,1024]{1,0:T(1,128)} %bitcast.9, s32[1,16]{1,0:T(1,128)} %docs_hbm.1), custom_call_target="tpu_custom_call" | custom-call | tf_op jit(solution)/shard_map/pallas_call | solution.py:534
  62.7 1.3 %copy.8 = bf16[1,256,4096]{2,1,0:T(8,128)(2,1)} copy(bf16[1,256,4096]{2,1,0:T(8,128)(2,1)S(1)} %bitcast.5) | data formatting | bytes 4194304

commit v4 on v3

--- a/solution.py
+++ b/solution.py
@@ -19,7 +19,8 @@
 SPLIT = 4
 LEAD = 6
 NEAR = 5
-SEATS = MSGS + 2 + SPLIT
+SEATS = 2 * MSGS
+HALVED = 4
 FIRST, SECOND, EARLY, LATE = range(4)
 XCH = 8
 QB = 128
@@ -37,7 +38,7 @@
     x_hbm, q_hbm, gain_hbm, w_hbm, vbias_hbm, docs_hbm,
     out,
     docs, x, q, res, gain, vbias, w, xs, xr, own, ps, pr, kv, mask,
-    local_sem, x_sem, wsem, xsend, xrecv, psend, precv, ssend, srecv, fsend, osem,
+    local_sem, x_sem, wsem, xsend, xrecv, psend, precv, ssend, srecv, arrived, fsend, osem,
     *gather,
 ):
     tokens, depth = x.shape
@@ -306,11 +307,16 @@
         LATE: (ahead, tokens - ahead),
     }
 
+    def cuts(m):
+        if m < SPLIT:
+            return (EARLY, LATE)
+        return (FIRST, SECOND) if m >= HALVED else (None,)
+
     def rows_of(piece):
         return pl.ds(*spans[piece])
 
     def seat(m, piece):
-        return m + {SECOND: 2, LATE: MSGS + 2}.get(piece, 0)
+        return m + (MSGS if piece in (SECOND, LATE) else 0)
 
     def psendcopy(o, m, piece):
         source = lax.rem(chip + chips - o, chips)
@@ -329,7 +335,7 @@
             for h in range(2):
                 ps[o - 1, 4 * j + 2 * h + kind, part, :] = partial[:, h * HD:(h + 1) * HD]
         for m in range(4 * j, 4 * j + 4):
-            for cut in (FIRST, SECOND) if m >= LAST else (piece,):
+            for cut in (piece,) if m < SPLIT else cuts(m):
                 psendcopy(o, m, cut).start()
 
     def slot(b, piece):
@@ -340,13 +346,14 @@
         k = seat(m, piece)
         return pltpu.make_async_remote_copy(
             kv.at[m, slot(0, piece)], kv.at[m, slot(b, piece)], ssend.at[b - 1],
-            srecv.at[b - 1, k], device_id={"sp": i + b},
+            srecv.at[k] if b == 2 else arrived.at[max(b - 2, 0), m // 2], device_id={"sp": i + b},
         )
 
     def relay(m, piece):
         k = seat(m, piece)
         return pltpu.make_async_remote_copy(
-            kv.at[m, slot(2, piece)], kv.at[m, slot(1, piece)], fsend.at[0], srecv.at[0, k],
+            kv.at[m, slot(2, piece)], kv.at[m, slot(1, piece)], fsend.at[0],
+            arrived.at[0, m // 2],
             device_id={"sp": i - 1},
         )
 
@@ -376,12 +383,12 @@
         def _():
             relay(m, piece).start()
 
-    def arrive(m, piece):
+    def arrive(g):
         for b in range(1, reach + 1):
             if b != 2:
                 @pl.when(i >= b)
                 def _():
-                    shiftcopy(b, m, piece).wait_recv()
+                    take(arrived.at[max(b - 2, 0), g], kv.at[pl.ds(2 * g, 2), slot(b, None)])
 
     factor = HD ** (-0.5) * math.log2(math.e)
     ratio = QH // KVH
@@ -421,11 +428,6 @@
         @pl.when(condition)
         def _():
             action()
-
-    def cuts(m):
-        if m < SPLIT:
-            return (EARLY, LATE)
-        return (FIRST, SECOND) if m >= LAST else (None,)
 
     def finish_all(messages, piece):
         for m in messages:
@@ -469,23 +471,27 @@
     finish(SPLIT - 1, EARLY)
     finish_all(range(SPLIT), LATE)
     pass_all(range(SPLIT), EARLY)
-    finish(SPLIT, None)
+    for cut in cuts(SPLIT):
+        finish(SPLIT, cut)
     pass_all(range(SPLIT), LATE)
 
     def serve(k, lead, relays):
-        if k + lead < MSGS:
-            for cut in cuts(k + lead):
-                finish(k + lead, cut)
-        if relays and SPLIT <= k + lead - 3 < MSGS:
-            for cut in cuts(k + lead - 3):
-                pass_on(k + lead - 3, cut)
-
-    when(i >= 2, lambda: finish_all(range(SPLIT + 1, LEAD), None))
-
-    def ready(g):
-        for m in (2 * g, 2 * g + 1):
+        for turn in range(2):
+            m = k + lead
+            if m < MSGS:
+                for cut in cuts(m)[turn:turn + 1]:
+                    finish(m, cut)
+            m = m - 3
+            if relays and SPLIT <= m < MSGS:
+                for cut in cuts(m)[turn:turn + 1]:
+                    pass_on(m, cut)
+
+    def start(lead):
+        for m in range(SPLIT + 1, lead):
             for cut in cuts(m):
-                arrive(m, cut)
+                finish(m, cut)
+
+    when(i >= 2, functools.partial(start, LEAD))
 
     for g in range(KVH):
         for u in range(tokens // QB):
@@ -493,7 +499,7 @@
             when(i >= 2, functools.partial(serve, k, LEAD, True))
             when(i < 2, functools.partial(serve, k, NEAR, False))
             if u == 0:
-                ready(g)
+                arrive(g)
             attend(g, u)
 
     for o in range(1, chips):
@@ -559,7 +565,8 @@
             dma((far,)),
             dma((far, SEATS)),
             dma((reach,)),
-            dma((reach, SEATS)),
+            dma((SEATS,)),
+            dma((max(reach - 1, 1), KVH)),
             dma((1,)),
             dma((1,)),
         ] + taken,

time: 64.2 us -> 63.7 us (level)
  no operation moved by 1% of the time
where the time goes in v4:
time: 63.7 us; the launch traced here: 63.6 us
  Pallas kernels  62.2 us (98%)
  local copies, waits for them, and re-layouts  1.32 us (2%)
    pallas_call x1, Pallas kernels, shards(): pl.pallas_call(functools.partial(kernel, n, s, reach, give), out_shape=ja...  62.2 us
    unnamed x1, local copies, waits for them, and re-layouts  1.32 us

profile of v4, /device:TPU:8, one launch (start us, length us, event | category | flops | bytes accessed | tf_op | source)
XLA Modules:
  0.0 63.6 jit_solution(1990171306183146048)
XLA Ops:
  0.0 62.2 %shard_map.64 = bf16[256,4096]{1,0:T(8,128)(2,1)S(1)} custom-call(bf16[256,5120]{1,0:T(8,128)(2,1)} %bitcast.6, bf16[256,4096]{1,0:T(8,128)(2,1)} %bitcast.7, f32[1,5120]{1,0:T(1,128)} %bitcast.8, bf16[1280,2048]{1,0:T(8,128)(2,1)} %w_hbm.1, f32[1,1024]{1,0:T(1,128)} %bitcast.9, s32[1,16]{1,0:T(1,128)} %docs_hbm.1), custom_call_target="tpu_custom_call" | custom-call | tf_op jit(solution)/shard_map/pallas_call | solution.py:540
  62.2 1.3 %copy.8 = bf16[1,256,4096]{2,1,0:T(8,128)(2,1)} copy(bf16[1,256,4096]{2,1,0:T(8,128)(2,1)S(1)} %bitcast.5) | data formatting | bytes 4194304
